TPU v7x, 32 devices: a whole 2x2x4 slice. The times are simulated.
32 devices in a mesh: blk: 8 (over y, x, core), grp: 4 (over z).
Axes of the slice: x: 2, y: 2, z: 4, core: 2. Of those that a mesh axis runs over, the one named last changes fastest.
Arguments:
- samples: float32 [32, 128, 256], P('blk', 'grp'), may hold values from -11 to 11
- pair_table: int32 [32, 16], P('blk'), may hold values from 0 to 31
- assignment: int32 [2, 32], P(None, 'blk'), may hold values from 0 to 127
- band_index: int32 [2], replicated, may hold values from 0 to 1023
Outputs:
- log_weight: float32 [2, 32, 128], P(None, 'blk', 'grp')
All inputs are finite; a program needn't handle non-finite values.
Results may differ from a plain program's by a relative error of at most 0.0003.
Values sent between devices are 32-bit elements; how exact they have to be, the bound alone decides.
No kernel may reach another device: no remote copies, remote signals or barrier semaphores. Data moves between devices by JAX's collectives and lax.ppermute only.
A program may use at most 128 MiB of HBM per device.

v0:
```python
import jax
import jax.numpy as jnp
from jax import lax
from jax.sharding import PartitionSpec as P

PAIRS = 16


def joined_2(shard, axis, combine):
    everything = jax.tree.map(lambda part: lax.all_gather(part, axis), shard)
    initial = jax.tree.map(lambda part: part[0], everything)

    def hop(k, so_far):
        return combine(so_far, jax.tree.map(lambda part: part[k], everything))

    return lax.fori_loop(1, lax.axis_size(axis), hop, initial)


def make_fold(queries, query_norm, band_list, counts):

    def fold(state, shard_rows, offset):
        count_in = shard_rows.shape[0]
        rows_dev = shard_rows.shape[1]

        def compute(inner):
            key_rows = shard_rows.reshape(count_in * rows_dev, shard_rows.shape[2])
            key_norm = jnp.sum(key_rows * key_rows, -1)
            product = jnp.einsum("qd,kd->qk", queries, key_rows, precision=lax.Precision.HIGHEST)
            distance = query_norm[:, None] + key_norm[None, :] - 2.0 * product
            blocks = []
            for band_sq in band_list:
                scores = (-distance / (2.0 * band_sq)).reshape(
                    distance.shape[0], count_in, rows_dev
                )
                peak = jnp.max(scores, -1)
                blocks.append(peak + jnp.log(jnp.sum(jnp.exp(scores - peak[..., None]), -1)))
            update = jnp.stack(blocks)
            return lax.dynamic_update_slice(inner, update, (0, 0, offset))

        needed = jnp.any(counts > 0)
        return lax.cond(needed, compute, lambda inner: inner, state)

    return fold


def per_device(samples, pair_table, assignment, band_index):
    local_subs, rows_dev, width = samples.shape
    rounds = assignment.shape[0]
    group_size = lax.axis_size("grp")
    group_index = lax.axis_index("grp")
    members = local_subs * lax.axis_size("blk")
    band_sq = width * (1.0 + band_index.astype(jnp.float32) / 256.0) / 32.0
    local_pick = assignment - group_index * rows_dev
    onehot = (
        local_pick[:, :, None] == jnp.arange(rows_dev, dtype=jnp.int32)[None, None, :]
    ).astype(jnp.float32)
    picked = jnp.einsum("tsr,srd->td", onehot, samples, precision=lax.Precision.HIGHEST)
    centre = lax.psum(picked, ("blk", "grp")) / members
    member_ids = jnp.arange(members, dtype=jnp.int32)
    count_int = jnp.sum(
        (pair_table[:, :, None] == member_ids[None, None, :]).astype(jnp.int32), axis=1
    )
    counts = count_int.astype(jnp.float32)
    gathered = lax.all_gather(samples, "grp", axis=1, tiled=True)
    query_count = local_subs * rows_dev * group_size
    queries = gathered.reshape(query_count, width)
    query_norm = jnp.sum(queries * queries, -1)
    start_state = jnp.zeros((rounds, query_count, members), jnp.float32)
    fold = make_fold(queries, query_norm, [band_sq[turn] for turn in range(rounds)], count_int)
    partial_value = fold(
        start_state, lax.all_gather(samples, "blk", axis=0, tiled=True), jnp.int32(0)
    )
    split_view = partial_value.reshape(rounds, local_subs, group_size, rows_dev, members)
    swapped = lax.all_to_all(split_view, "grp", split_axis=2, concat_axis=2, tiled=True)
    peak = jnp.max(swapped, 2)
    kernel = peak + jnp.log(jnp.sum(jnp.exp(swapped - peak[:, :, None]), 2))
    weighted = jnp.einsum("tsrm,sm->tsr", kernel, counts, precision=lax.Precision.HIGHEST) / PAIRS
    spread = samples[None] - centre[:, None, None, :]
    logits = weighted - jnp.sum(spread * spread, -1) / (2.0 * band_sq[:, None, None])
    row_peak = jnp.max(logits, -1)
    row_total = jnp.sum(jnp.exp(logits - row_peak[..., None]), -1)

    def combine_pair(first, second):
        joined = jnp.maximum(first[0], second[0])
        return (
            joined,
            first[1] * jnp.exp(first[0] - joined) + second[1] * jnp.exp(second[0] - joined),
        )

    peak_all, total_all = joined_2((row_peak, row_total), "grp", combine_pair)
    return logits - peak_all[..., None] - jnp.log(total_all)[..., None]


def solution(mesh):
    return jax.shard_map(
        per_device,
        mesh=mesh,
        in_specs=(P("blk", "grp", None), P("blk", None), P(None, "blk"), P()),
        out_specs=P(None, "blk", "grp"),
        check_vma=False,
    )
```

profile of v0, /device:TPU:0, one launch (start us, length us, event | category | flops | bytes accessed | tf_op | source)
XLA Modules:
  0.0 123.1 jit_solution(9642932200936565193)
XLA Ops:
  6.5 0.0 all-gather.6.cloned.1.call-start
  6.5 0.7 all-gather.6.cloned.1.call-update
  7.3 0.8 convert_reduce_fusion
  8.0 0.6 compare_reduce_fusion
  9.3 0.7 broadcast_subtract_fusion
  10.0 0.1 copy.19
  10.1 1.2 convolution_bitcast_fusion
  11.3 42.0 %psum.7 = f32[2,256]{1,0:T(2,128)S(1)} all-reduce(f32[2,256]{1,0:T(2,128)S(1)} %convolution_bitcast_fusion), channel_id=1, replica_groups=mesh['blk'=8,'grp'=4] {'blk','grp'}, use_global_device_ids=true, to_apply=%region_12.0 | all-reduce | flops 512 | bytes 4096 | tf_op jit(solution)/shard_map/psum | solution.py:58
  53.2 15.9 %all_gather.18 = f32[4,128,256]{2,1,0:T(8,128)S(1)} all-gather(f32[4,32,256]{2,1,0:T(8,128)} %param.8), channel_id=1, replica_groups=mesh['blk'=8,'grp'=4] {'grp'}, dimensions={1}, use_global_device_ids=true | all-gather | bytes 655360 | tf_op jit(solution)/shard_map/all_gather | solution.py:64
  69.2 0.7 multiply_add_fusion
  69.8 0.0 all-gather.6.cloned.1.call-done
  69.8 14.7 %conditional.1 = (f32[2,512,32]{1,2,0:T(8,128)S(1)}) conditional(s32[]{:T(128)} %convert_element_type.15, () %tuple.36, (f32[4,128,256]{2,1,0:T(8,128)S(1)}, f32[32,32,256]{2,1,0:T(8,128)}, f32[2]{0:T(128)S(1)}) %tuple.37), branch_computations={%region_2.0_spmd, %region_3.10_spmd} | conditional | flops 1617689088 | bytes 25186376 | solution.py:41
  69.8 1.4 %multiply_reduce_fusion = f32[32,32]{1,0:T(8,128)S(1)} fusion(f32[32,32,256]{2,1,0:T(8,128)} %get-tuple-element.164), kind=kLoop, calls=%fused_computation.11 | loop fusion | flops 523264 | bytes 1052672 | tf_op jit(solution)/shard_map/cond/branch_1_fun/reduce_sum | solution.py:27
  71.3 0.1 add.87
  71.3 0.7 fusion.12
  73.4 0.1 multiply_reduce_fusion.1
  73.5 5.3 %broadcast_divide_fusion.1 = (f32[512,1024]{1,0:T(8,128)}, f32[512,1024]{1,0:T(8,128)}) fusion(f32[]{:T(128)} %bitcast.3, f32[]{:T(128)} %bitcast.6, f32[512,256]{1,0:T(8,128)S(1)} %bitcast.71, f32[1024,256]{1,0:T(8,128)} %bitcast.74, f32[1024]{0:T(1024)S(1)} %add.87, f32[512]{0:T(512)S(1)} %bitcast.80), kind=kOutput, calls=%fused_computation.10 | convolution fusion | flops 1613758464 | bytes 5773320 | tf_op jit(solution)/shard_map/cond/branch_1_fun/qd,kd->qk/dot_general | solution.py:28
  78.8 1.9 %copy.16 = f32[512,1024]{0,1:T(8,128)S(1)} copy(f32[512,1024]{1,0:T(8,128)} %get-tuple-element.190) | data formatting | bytes 4194304 | tf_op jit(solution)/shard_map/cond/branch_1_fun/div | solution.py:32
  80.8 0.3 bitcast_reduce_fusion.1
  81.1 0.5 fusion.3
  81.6 1.9 %copy.17 = f32[512,1024]{0,1:T(8,128)S(1)} copy(f32[512,1024]{1,0:T(8,128)} %get-tuple-element.191) | data formatting | bytes 4194304 | tf_op jit(solution)/shard_map/cond/branch_1_fun/div | solution.py:32
  83.6 0.3 bitcast_reduce_fusion
  83.9 0.5 fusion.1
  84.5 0.0 copy-start
  84.5 0.3 reshape.79
  84.8 0.1 copy.28
  84.9 1.0 reshape.97
  85.9 3.8 %all-to-all-start = ((f32[4,1,8192]{2,1,0:T(1,128)}), f32[4,1,8192]{2,1,0:T(1,128)S(1)}, u32[]{:S(2)}, u32[]{:S(2)}) async-start(f32[4,1,8192]{2,1,0:T(1,128)} %reshape.97), calls=%async_computation | async-start | bytes 262144 | tf_op jit(solution)/shard_map/all_to_all | solution.py:74
  89.7 0.0 copy-done
  89.7 0.1 multiply_reduce_fusion.2
  89.8 5.8 %all-to-all-done = f32[4,1,8192]{2,1,0:T(1,128)S(1)} async-done(((f32[4,1,8192]{2,1,0:T(1,128)}), f32[4,1,8192]{2,1,0:T(1,128)S(1)}, u32[]{:S(2)}, u32[]{:S(2)}) %all-to-all-start) | async-done | bytes 131104 | tf_op jit(solution)/shard_map/all_to_all | solution.py:74
  95.6 0.5 broadcast.44
  96.1 1.0 reduce.5
  97.1 0.3 reshape.98
  97.4 0.1 bitcast_reduce_fusion.2
  97.6 0.2 exponential_reduce_fusion
  97.8 0.2 fusion.6
  98.0 0.2 fusion.11
  98.2 0.2 exponential_reduce_fusion.1
  98.3 9.0 %all-gather.3 = f32[4,2,4]{2,1,0:T(2,128)S(1)} all-gather(f32[1,2,4]{2,1,0:T(2,128)S(1)} %bitcast.79), channel_id=3, replica_groups=mesh['blk'=8,'grp'=4] {'grp'}, dimensions={0}, use_global_device_ids=true | all-gather | bytes 160 | tf_op jit(solution)/shard_map/all_gather | solution.py:10
  107.3 8.2 %all-gather.2 = f32[4,2,4]{2,1,0:T(2,128)S(1)} all-gather(f32[1,2,4]{2,1,0:T(2,128)S(1)} %bitcast.77), channel_id=2, replica_groups=mesh['blk'=8,'grp'=4] {'grp'}, dimensions={0}, use_global_device_ids=true | all-gather | bytes 160 | tf_op jit(solution)/shard_map/all_gather | solution.py:10
  115.5 0.1 while.17
  115.6 0.7 subtract_subtract_fusion
  (12 shorter events, 0.2 us)
Async XLA Ops:
  6.5 63.3 %all-gather.6.cloned.1.call-start = ((), (), s32[]{:S(2)}) async-start(), calls=%async_computation.1 | async-start | bytes 1179648 | tf_op jit(solution)/shard_map/all_gather | solution.py:71
  84.5 5.2 %copy-start = (f32[4,32,256]{2,1,0:T(8,128)S(1)}, f32[4,32,256]{2,1,0:T(8,128)}, u32[]{:S(2)}) copy-start(f32[4,32,256]{2,1,0:T(8,128)} %param.8) | copy-start | bytes 393220
  85.9 9.7 %all-to-all-start = ((f32[4,1,8192]{2,1,0:T(1,128)}), f32[4,1,8192]{2,1,0:T(1,128)S(1)}, u32[]{:S(2)}, u32[]{:S(2)}) async-start(f32[4,1,8192]{2,1,0:T(1,128)} %reshape.97), calls=%async_computation | async-start | bytes 262144 | tf_op jit(solution)/shard_map/all_to_all | solution.py:74
Sparse Core Ops, SparseCore 0:
  9.2 26.2 all-gather.5
where the time goes:
time: 124 us; the launch traced here: 123 us
  blocking collectives  75 us (60%)
  between operations  14.1 us (11%)
  other arithmetic  8.66 us (7%)
  local copies, waits for them, and re-layouts  6.86 us (6%)
  matrix products  6.7 us (5%)
  waiting for transfers between devices  6.5 us (5%)
  starting transfers between devices  3.8 us (3%)
  loops' own time  1.43 us (1%)
    psum x1, blocking collectives, per_device(): centre = lax.psum(picked, ('blk', 'grp')) / members  42 us
    all_gather x2, blocking collectives, joined_2(): everything = jax.tree.map(lambda part: lax.all_gather(part, axis), shard)  17.2 us
    all_gather x1, blocking collectives, per_device(): gathered = lax.all_gather(samples, 'grp', axis=1, tiled=True)  15.9 us
    all_to_all x1, waiting for transfers between devices, per_device(): lax.all_to_all(split_view, 'grp', split_axis=2, concat_axis=2, tiled=True)  5.79 us
    dot_general x1, matrix products, compute(): jnp.einsum('qd,kd->qk', queries, key_rows, precision=lax.Precision.HIGHEST)  5.35 us
    div x2, local copies, waits for them, and re-layouts, compute(): -distance / (2.0 * band_sq)  3.84 us
    all_to_all x1, starting transfers between devices, per_device(): lax.all_to_all(split_view, 'grp', split_axis=2, concat_axis=2, tiled=True)  3.8 us
  transfers between devices with their start and end apart: 2, of which 1 were waited for; matrix products, arithmetic and copies ran while one was open for 3% of the time, Pallas kernels for 0%

commit v1 on v0

--- a/solution.py
+++ b/solution.py
@@ -55,7 +55,7 @@
         local_pick[:, :, None] == jnp.arange(rows_dev, dtype=jnp.int32)[None, None, :]
     ).astype(jnp.float32)
     picked = jnp.einsum("tsr,srd->td", onehot, samples, precision=lax.Precision.HIGHEST)
-    centre = lax.psum(picked, ("blk", "grp")) / members
+    centre = jnp.sum(lax.all_gather(picked, ("blk", "grp")), axis=0) / members
     member_ids = jnp.arange(members, dtype=jnp.int32)
     count_int = jnp.sum(
         (pair_table[:, :, None] == member_ids[None, None, :]).astype(jnp.int32), axis=1

time: 124 us -> 152 us (1.23)
  blocking collectives: 75 us -> 104 us
    all_gather x0 -> x1, blocking collectives: none -> 70.3 us  [per_device(): centre = jnp.sum(lax.all_gather(picked, ('blk', 'grp')), axis=0) / members]
    psum x1 -> x0, blocking collectives: 42 us -> none  [per_device(): centre = lax.psum(picked, ('blk', 'grp')) / members]
where the time goes in v1:
time: 152 us; the launch traced here: 151 us
  blocking collectives  104 us (68%)
  between operations  14.2 us (9%)
  other arithmetic  8.71 us (6%)
  local copies, waits for them, and re-layouts  6.86 us (5%)
  matrix products  6.7 us (4%)
  waiting for transfers between devices  6.45 us (4%)
  starting transfers between devices  3.32 us (2%)
    all_gather x1, blocking collectives, per_device(): centre = jnp.sum(lax.all_gather(picked, ('blk', 'grp')), axis=0) / members  70.3 us
    all_gather x2, blocking collectives, joined_2(): everything = jax.tree.map(lambda part: lax.all_gather(part, axis), shard)  17.2 us
    all_gather x1, blocking collectives, per_device(): gathered = lax.all_gather(samples, 'grp', axis=1, tiled=True)  16.1 us
    all_to_all x1, waiting for transfers between devices, per_device(): lax.all_to_all(split_view, 'grp', split_axis=2, concat_axis=2, tiled=True)  5.73 us
    dot_general x1, matrix products, compute(): jnp.einsum('qd,kd->qk', queries, key_rows, precision=lax.Precision.HIGHEST)  5.35 us
    div x2, local copies, waits for them, and re-layouts, compute(): -distance / (2.0 * band_sq)  3.84 us
    all_to_all x1, starting transfers between devices, per_device(): lax.all_to_all(split_view, 'grp', split_axis=2, concat_axis=2, tiled=True)  3.32 us
  transfers between devices with their start and end apart: 2, of which 1 were waited for; matrix products, arithmetic and copies ran while one was open for 3% of the time, Pallas kernels for 0%

profile of v1, /device:TPU:0, one launch (start us, length us, event | category | flops | bytes accessed | tf_op | source)
XLA Modules:
  0.0 151.2 jit_solution(4682284197212759445)
XLA Ops:
  6.5 0.0 all-gather.8.cloned.1.call-start
  6.5 0.7 all-gather.8.cloned.1.call-update
  7.3 0.8 convert_reduce_fusion
  8.0 0.6 compare_reduce_fusion
  9.3 0.7 broadcast_subtract_fusion
  10.0 0.1 copy.19
  10.1 1.2 convolution_bitcast_fusion
  11.3 70.3 %all-gather.3 = f32[32,2,256]{2,1,0:T(2,128)S(1)} all-gather(f32[1,2,256]{2,1,0:T(2,128)S(1)} %convolution_bitcast_fusion), channel_id=2, replica_groups=mesh['blk'=8,'grp'=4] {'blk','grp'}, dimensions={0}, use_global_device_ids=true | all-gather | bytes 67584 | tf_op jit(solution)/shard_map/all_gather | solution.py:58
  81.6 16.1 %all_gather.24 = f32[4,128,256]{2,1,0:T(8,128)S(1)} all-gather(f32[4,32,256]{2,1,0:T(8,128)} %param.8), channel_id=1, replica_groups=mesh['blk'=8,'grp'=4] {'grp'}, dimensions={1}, use_global_device_ids=true | all-gather | bytes 655360 | tf_op jit(solution)/shard_map/all_gather | solution.py:64
  97.7 0.7 multiply_add_fusion
  98.4 0.0 all-gather.8.cloned.1.call-done
  98.4 14.7 %conditional.1 = (f32[2,512,32]{1,2,0:T(8,128)S(1)}) conditional(s32[]{:T(128)} %convert_element_type.15, () %tuple.36, (f32[4,128,256]{2,1,0:T(8,128)S(1)}, f32[32,32,256]{2,1,0:T(8,128)}, f32[2]{0:T(128)S(1)}) %tuple.37), branch_computations={%region_2.0_spmd, %region_3.10_spmd} | conditional | flops 1617689088 | bytes 25186376 | solution.py:41
  98.4 1.4 multiply_reduce_fusion
  99.8 0.1 add.85
  99.9 0.7 fusion.12
  101.9 0.1 multiply_reduce_fusion.1
  102.1 5.3 %broadcast_divide_fusion.1 = (f32[512,1024]{1,0:T(8,128)}, f32[512,1024]{1,0:T(8,128)}) fusion(f32[]{:T(128)} %bitcast.3, f32[]{:T(128)} %bitcast.6, f32[512,256]{1,0:T(8,128)S(1)} %bitcast.72, f32[1024,256]{1,0:T(8,128)} %bitcast.75, f32[1024]{0:T(1024)S(1)} %add.85, f32[512]{0:T(512)S(1)} %bitcast.81), kind=kOutput, calls=%fused_computation.10 | convolution fusion | flops 1613758464 | bytes 5773320 | tf_op jit(solution)/shard_map/cond/branch_1_fun/qd,kd->qk/dot_general | solution.py:28
  107.4 1.9 %copy.16 = f32[512,1024]{0,1:T(8,128)S(1)} copy(f32[512,1024]{1,0:T(8,128)} %get-tuple-element.190) | data formatting | bytes 4194304 | tf_op jit(solution)/shard_map/cond/branch_1_fun/div | solution.py:32
  109.3 0.3 bitcast_reduce_fusion.1
  109.7 0.5 fusion.3
  110.2 1.9 %copy.17 = f32[512,1024]{0,1:T(8,128)S(1)} copy(f32[512,1024]{1,0:T(8,128)} %get-tuple-element.191) | data formatting | bytes 4194304 | tf_op jit(solution)/shard_map/cond/branch_1_fun/div | solution.py:32
  112.1 0.3 bitcast_reduce_fusion
  112.5 0.5 fusion.1
  113.1 0.0 copy-start
  113.1 0.3 reshape.81
  113.3 0.1 copy.28
  113.5 1.0 reshape.103
  114.5 3.3 %all-to-all-start = ((f32[4,1,8192]{2,1,0:T(1,128)}), f32[4,1,8192]{2,1,0:T(1,128)S(1)}, u32[]{:S(2)}, u32[]{:S(2)}) async-start(f32[4,1,8192]{2,1,0:T(1,128)} %reshape.103), calls=%async_computation | async-start | bytes 262144 | tf_op jit(solution)/shard_map/all_to_all | solution.py:74
  117.8 0.0 copy-done
  117.8 0.1 multiply_reduce_fusion.2
  118.0 5.7 %all-to-all-done = f32[4,1,8192]{2,1,0:T(1,128)S(1)} async-done(((f32[4,1,8192]{2,1,0:T(1,128)}), f32[4,1,8192]{2,1,0:T(1,128)S(1)}, u32[]{:S(2)}, u32[]{:S(2)}) %all-to-all-start) | async-done | bytes 131104 | tf_op jit(solution)/shard_map/all_to_all | solution.py:74
  123.7 0.5 broadcast.47
  124.2 1.0 reduce.6
  125.2 0.3 reshape.104
  125.5 0.1 bitcast_reduce_fusion.2
  125.6 0.2 exponential_reduce_fusion
  125.9 0.2 fusion.6
  126.1 0.2 fusion.11
  126.2 0.2 exponential_reduce_fusion.1
  126.4 9.0 %all-gather.5 = f32[4,2,4]{2,1,0:T(2,128)S(1)} all-gather(f32[1,2,4]{2,1,0:T(2,128)S(1)} %bitcast.80), channel_id=4, replica_groups=mesh['blk'=8,'grp'=4] {'grp'}, dimensions={0}, use_global_device_ids=true | all-gather | bytes 160 | tf_op jit(solution)/shard_map/all_gather | solution.py:10
  135.4 8.2 %all-gather.4 = f32[4,2,4]{2,1,0:T(2,128)S(1)} all-gather(f32[1,2,4]{2,1,0:T(2,128)S(1)} %bitcast.78), channel_id=3, replica_groups=mesh['blk'=8,'grp'=4] {'grp'}, dimensions={0}, use_global_device_ids=true | all-gather | bytes 160 | tf_op jit(solution)/shard_map/all_gather | solution.py:10
  143.6 0.1 while.17
  143.7 0.7 subtract_subtract_fusion
  (13 shorter events, 0.2 us)
Async XLA Ops:
  6.5 91.9 %all-gather.8.cloned.1.call-start = ((), (), s32[]{:S(2)}) async-start(), calls=%async_computation.1 | async-start | bytes 1179648 | tf_op jit(solution)/shard_map/all_gather | solution.py:71
  113.1 4.8 %copy-start = (f32[4,32,256]{2,1,0:T(8,128)S(1)}, f32[4,32,256]{2,1,0:T(8,128)}, u32[]{:S(2)}) copy-start(f32[4,32,256]{2,1,0:T(8,128)} %param.8) | copy-start | bytes 393220
  114.5 9.2 %all-to-all-start = ((f32[4,1,8192]{2,1,0:T(1,128)}), f32[4,1,8192]{2,1,0:T(1,128)S(1)}, u32[]{:S(2)}, u32[]{:S(2)}) async-start(f32[4,1,8192]{2,1,0:T(1,128)} %reshape.103), calls=%async_computation | async-start | bytes 262144 | tf_op jit(solution)/shard_map/all_to_all | solution.py:74
Sparse Core Ops, SparseCore 0:
  9.2 26.1 all-gather.7
